TPU v7x, 32 devices: a whole 2x2x4 slice. The times are simulated.
32 devices in a mesh: leaf: 8 (over y, x, core), group: 4 (over z).
Axes of the slice: x: 2, y: 2, z: 4, core: 2. Of those that a mesh axis runs over, the one named last changes fastest.
Arguments:
- coefficients: float32 [4, 4096, 512], P('group', 'leaf'), may hold values from -6 to 6
- labels: float32 [4, 4096, 512], P('group', 'leaf'), may hold values from -6 to 6
- near_kernel: float32 [4, 4096, 3072], P('group', 'leaf'), may hold values from -0.109375 to 0.109375
- basis: float32 [4, 4096, 256], P('group', 'leaf'), may hold values from -0.1875 to 0.1875
- transfer: float32 [4, 1024, 256], P('group', 'leaf'), may hold values from -0.375 to 0.375
- coupling: float32 [4, 256, 1024], P('group', 'leaf'), may hold values from -0.1875 to 0.1875
- near_lists: int32 [4, 4, 3], P('group'), may hold values from 0 to 3, as said below
- ridge: float32 [1], replicated, may hold values from 0.5 to 2
Outputs:
- residual: float32 [4, 4096, 512], P('group', 'leaf')
Inputs may be any that keep to these rules, and one draw needn't show every extreme that they name: `near_lists`: entry 0 of each leaf's list is the leaf itself; in each group the leaves lie on one cycle through all 4 leaves, and entries 1 and 2 of a leaf's list are its two neighbours on that cycle.
All inputs are finite; a program needn't handle non-finite values.
Results may differ from a plain program's by a relative error of at most 0.0011.
Values may be sent and summed in bfloat16 or wider, within the bound.
No kernel may reach another device: no remote copies, remote signals or barrier semaphores. Data moves between devices by JAX's collectives and lax.ppermute only.
A program may use at most 64 MiB of HBM per device.

v0:
```python
import jax
import jax.numpy as jnp
from jax import lax
from jax.sharding import PartitionSpec as P

LPG = 4


def swapped(shard, axis, distance):
    return lax.ppermute(shard, axis, [(i, i ^ 1 << distance) for i in range(lax.axis_size(axis))])


def matmul(left, right):
    return jnp.dot(left, right, precision=lax.Precision.HIGHEST, preferred_element_type=jnp.float32)


def shards(coefficients, labels, near_kernel, basis, transfer, coupling, near_lists, ridge):
    local_coef = coefficients[0]
    column_count = local_coef.shape[1]
    leaf_split = lax.axis_size("leaf") // LPG
    levels = leaf_split.bit_length() - 1
    position = lax.axis_index("leaf")
    leaf_index = position // leaf_split
    chosen = lax.dynamic_index_in_dim(near_lists[0], leaf_index, 0, keepdims=False)
    local_kernel = near_kernel[0]
    list_length = chosen.shape[0]
    leaf_width = local_kernel.shape[1] // list_length
    group_all = lax.all_gather(coefficients, "leaf", axis=1, tiled=True)[0]
    leaf_blocks = group_all.reshape(group_all.shape[0] // leaf_width, leaf_width, column_count)
    selected = jnp.take(leaf_blocks, chosen, axis=0)
    near = matmul(local_kernel, selected.reshape(list_length * leaf_width, column_count))
    basis_rows = basis[0]
    partial_coef = matmul(basis_rows.T, local_coef)
    for bit_level in reversed(range(levels)):
        halfway = partial_coef.shape[0] // 2
        lower_half = partial_coef[:halfway]
        upper_half = partial_coef[halfway:]
        upper_side = position // (1 << bit_level) % 2 == 1
        kept = jnp.where(upper_side, upper_half, lower_half)
        given = jnp.where(upper_side, lower_half, upper_half)
        partial_coef = kept + swapped(given, "leaf", bit_level)
    contribution = matmul(transfer[0].T, partial_coef)
    coupling_rows = coupling[0]
    group_coef = lax.psum(contribution, "leaf")
    group_round = group_coef.astype(jnp.bfloat16)
    coarse_part = matmul(
        coupling_rows, lax.all_gather(group_round, "group", axis=0, tiled=True).astype(jnp.float32)
    )
    coarse = lax.all_gather(coarse_part, "leaf", axis=0, tiled=True)
    slice_coarse = matmul(transfer[0], coarse)
    for bit_level in range(levels):
        partner = swapped(slice_coarse, "leaf", bit_level)
        upper_side = position // (1 << bit_level) % 2 == 1
        slice_coarse = jnp.where(
            upper_side,
            jnp.concatenate([partner, slice_coarse], axis=0),
            jnp.concatenate([slice_coarse, partner], axis=0),
        )
    far = matmul(basis_rows, slice_coarse)
    result = labels[0] - (near + far + ridge[0] * local_coef)
    return result[None]


def solution(mesh):
    return jax.shard_map(
        shards,
        mesh=mesh,
        in_specs=(
            P("group", "leaf", None),
            P("group", "leaf", None),
            P("group", "leaf", None),
            P("group", "leaf", None),
            P("group", "leaf", None),
            P("group", "leaf", None),
            P("group", None, None),
            P(),
        ),
        out_specs=P("group", "leaf", None),
        check_vma=False,
    )
```

profile of v0, /device:TPU:0, one launch (start us, length us, event | category | flops | bytes accessed | tf_op | source)
XLA Modules:
  0.0 172.0 jit_solution(16874923085528226704)
XLA Ops:
  6.5 0.0 copy-start
  6.5 0.0 copy-start.1
  6.5 0.0 copy-start.5
  6.5 0.0 copy-start.4
  6.5 0.0 copy-start.7
  6.5 0.0 copy-start.6
  6.6 0.0 all-gather.5.cloned.1.call-start
  6.6 1.3 copy-done
  7.9 2.3 %fusion.6 = f32[256,512]{1,0:T(8,128)S(1)} fusion(f32[1,512,512]{2,1,0:T(8,128)} %param.8, f32[1,512,256]{2,1,0:T(8,128)S(1)} %copy-done), kind=kOutput, calls=%fused_computation.12 | convolution fusion | flops 805306368 | bytes 2097152 | tf_op jit(solution)/shard_map/dot_general | solution.py:14
  10.3 0.6 collective-permute-start
  10.8 1.2 collective-permute-done
  12.0 1.5 convolution_bitcast_fusion
  13.5 32.9 %all-reduce.1 = bf16[256,512]{0,1:T(8,128)(2,1)} all-reduce(f32[256,512]{0,1:T(8,128)S(1)} %convolution_bitcast_fusion), channel_id=1, replica_groups=mesh['leaf'=8,'group'=4] {'leaf'}, use_global_device_ids=true, to_apply=%region_0.1 | all-reduce | flops 131072 | bytes 786432 | tf_op jit(solution)/shard_map/psum | solution.py:44
  46.4 0.0 all-gather.5.cloned.1.call-update
  46.4 0.0 all-gather.3.cloned.1.call-start
  46.5 0.7 all-gather.3.cloned.1.call-update
  47.2 0.0 copy-done.1
  47.2 1.3 copy.16
  49.2 0.0 copy-done.4
  49.2 1.3 copy.15
  50.5 0.0 copy-done.7
  50.5 0.2 dynamic-slice_reduce_fusion
  50.8 25.1 %all-gather.5.cloned.1.call-done = bf16[1024,512]{0,1:T(8,128)(2,1)} async-done(((bf16[256,512]{0,1:T(8,128)(2,1)}), bf16[1024,512]{0,1:T(8,128)(2,1)}) %all-gather.5.cloned.1.call-update) | async-done | bytes 1048592 | tf_op jit(solution)/shard_map/all_gather | solution.py:47
  75.9 0.0 copy-done.6
  75.9 2.2 %convolution_bitcast_fusion.2 = f32[32,512]{1,0:T(8,128)S(1)} fusion(bf16[1024,512]{0,1:T(8,128)(2,1)} %all-gather.5.cloned.1.call-done, f32[1,32,1024]{2,1,0:T(8,128)S(1)} %copy-done.6), kind=kOutput, calls=%fused_computation.11 | convolution fusion | flops 201326592 | bytes 1245184 | tf_op jit(solution)/shard_map/dot_general | solution.py:14
  78.1 9.2 %all_gather.11 = f32[256,512]{1,0:T(8,128)S(1)} all-gather(f32[32,512]{1,0:T(8,128)S(1)} %convolution_bitcast_fusion.2), channel_id=1, replica_groups=mesh['leaf'=8,'group'=4] {'leaf'}, dimensions={0}, use_global_device_ids=true | all-gather | bytes 589824 | tf_op jit(solution)/shard_map/all_gather | solution.py:49
  87.3 0.0 copy-done.5
  87.3 0.4 convolution_bitcast_fusion.1
  87.8 0.4 collective-permute-start.1
  88.2 42.1 %all-gather.3.cloned.1.call-done = f32[1,4096,512]{2,1,0:T(8,128)} async-done(((f32[1,512,512]{2,1,0:T(8,128)}), f32[1,4096,512]{2,1,0:T(8,128)}) %all-gather.3.cloned.1.call-update) | async-done | bytes 8388624 | tf_op jit(solution)/shard_map/all_gather | solution.py:28
  130.4 0.0 slice-start
  130.4 7.2 %gather_fusion = f32[3,1024,512]{2,1,0:T(8,128)} fusion(f32[4,1024,512]{2,1,0:T(8,128)} %bitcast.55, s32[1024]{0:T(1024)S(1)} %pad_clamp_fusion), kind=kCustom, calls=%fused_computation | custom fusion | bytes 12582924 | tf_op jit(solution)/shard_map/jit(_take)/gather | solution.py:30
  137.5 0.0 slice-start.1
  137.5 3.8 %broadcast_select_fusion = f32[3,1024,512]{2,1,0:T(8,128)S(1)} fusion(f32[3,1024,512]{2,1,0:T(8,128)} %gather_fusion, pred[3]{0:T(512)(128)(4,1)S(1)} %compare_and_fusion), kind=kLoop, calls=%fused_computation.3 | loop fusion | flops 1572864 | bytes 12582915 | tf_op jit(solution)/shard_map/jit(_take)/select_n | solution.py:30
  141.3 0.0 slice-done
  141.3 0.2 slice-done.1
  141.5 0.0 copy-start.2
  141.5 0.0 copy-start.3
  141.5 20.3 %fusion = f32[512,512]{1,0:T(8,128)S(1)} fusion(f32[3072,512]{1,0:T(8,128)S(1)} %bitcast.52, f32[1,512,3072]{2,1,0:T(8,128)S(1)} %bitcast.54), kind=kOutput, calls=%fused_computation.1 | convolution fusion | flops 9663676416 | bytes 13631488 | tf_op jit(solution)/shard_map/dot_general | solution.py:14
  161.9 0.0 collective-permute-done.1
  161.9 0.0 copy-done.2
  161.9 0.0 copy-done.3
  161.9 1.9 %fusion.5 = f32[1,512,512]{1,2,0:T(8,128)S(1)} fusion(f32[512,512]{1,0:T(8,128)S(1)} %fusion, f32[1,512,512]{1,2,0:T(8,128)S(1)} %copy-done.2, f32[1,512,512]{1,2,0:T(8,128)S(1)} %copy-done.3, f32[128,512]{1,0:T(8,128)S(1)} %convolution_bitcast_fusion.1, f32[128,512]{1,0:T(8,128)S(1)} %collective-permute-done.1, f32[1,512,256]{2,1,0:T(8,128)S(1)} %copy-done, ...), kind=kOutput, calls=%fused_computation.8 | convolution fusion | flops 806748160 | bytes 5242885 | tf_op jit(solution)/shard_map/dot_general | solution.py:14
  163.8 1.3 copy.17
  (5 shorter events, 0.1 us)
Async XLA Ops:
  6.5 1.4 copy-start
  6.5 40.7 %copy-start.1 = (f32[1,512,512]{2,1,0:T(8,128)S(1)}, f32[1,512,512]{2,1,0:T(8,128)}, u32[]{:S(2)}) copy-start(f32[1,512,512]{2,1,0:T(8,128)} %param.8) | copy-start | bytes 3145732
  6.5 80.8 %copy-start.5 = (f32[1,128,256]{2,1,0:T(8,128)S(1)}, f32[1,128,256]{2,1,0:T(8,128)}, u32[]{:S(2)}) copy-start(f32[1,128,256]{2,1,0:T(8,128)} %param.12) | copy-start | bytes 393220
  6.5 42.6 %copy-start.4 = (f32[1,512,512]{2,1,0:T(8,128)S(1)}, f32[1,512,512]{2,1,0:T(8,128)}, u32[]{:S(2)}) copy-start(f32[1,512,512]{2,1,0:T(8,128)} %param.9) | copy-start | bytes 3145732
  6.5 44.0 %copy-start.7 = (s32[1,4,3]{1,0,2:T(1,128)S(1)}, s32[1,4,3]{1,0,2:T(1,128)}, u32[]{:S(2)}) copy-start(s32[1,4,3]{1,0,2:T(1,128)} %param.14) | copy-start | bytes 148
  6.5 69.3 %copy-start.6 = (f32[1,32,1024]{2,1,0:T(8,128)S(1)}, f32[1,32,1024]{2,1,0:T(8,128)}, u32[]{:S(2)}) copy-start(f32[1,32,1024]{2,1,0:T(8,128)} %param.13) | copy-start | bytes 393220
  6.6 69.3 %all-gather.5.cloned.1.call-start = ((), (), s32[]{:S(2)}) async-start(), calls=%async_computation.1 | async-start | bytes 1310720 | tf_op jit(solution)/shard_map/all_gather | solution.py:47
  10.3 1.7 collective-permute-start
  46.4 83.9 %all-gather.3.cloned.1.call-start = ((), (), s32[]{:S(2)}) async-start(), calls=%async_computation | async-start | bytes 9437184 | tf_op jit(solution)/shard_map/all_gather | solution.py:28
  87.8 74.1 %collective-permute-start.1 = (f32[128,512]{1,0:T(8,128)S(1)}, f32[128,512]{1,0:T(8,128)S(1)}, u32[]{:S(2)}, u32[]{:S(2)}) collective-permute-start(f32[128,512]{1,0:T(8,128)S(1)} %convolution_bitcast_fusion.1), channel_id=1, source_target_pairs={{0,4},{4,0},{8,12},{12,8},{16,20},{20,16},{24,28},{28,24},{1,5},{5... | collective-permute-start | bytes 786440 | tf_op jit(solution)/shard_map/ppermute | solution.py:10
  130.4 11.0 %slice-start = ((s8[6291456]{0:T(1024)(128)(4,1)}), s8[2097152]{0:T(1024)(128)(4,1)S(1)}, s32[]{:S(2)}) async-start(s8[6291456]{0:T(1024)(128)(4,1)} %bitcast.53), calls=%async_computation.2 | async-start | bytes 4194304
  137.5 4.0 %slice-start.1 = ((s8[6291456]{0:T(1024)(128)(4,1)}), s8[4194304]{0:T(1024)(128)(4,1)S(1)}, s32[]{:S(2)}) async-start(s8[6291456]{0:T(1024)(128)(4,1)} %bitcast.53), calls=%async_computation.3 | async-start | bytes 8388608
  141.5 20.3 %copy-start.2 = (f32[1,512,512]{1,2,0:T(8,128)S(1)}, f32[1,512,512]{1,2,0:T(8,128)}, u32[]{:S(2)}) copy-start(f32[1,512,512]{1,2,0:T(8,128)} %copy.16) | copy-start | bytes 3145732
  141.5 20.4 %copy-start.3 = (f32[1,512,512]{1,2,0:T(8,128)S(1)}, f32[1,512,512]{1,2,0:T(8,128)}, u32[]{:S(2)}) copy-start(f32[1,512,512]{1,2,0:T(8,128)} %copy.15) | copy-start | bytes 3145732
Sparse Core Ops, SparseCore 0:
  46.6 29.2 all-gather.4
  77.8 52.5 all-gather.2
where the time goes:
time: 172 us
  waiting for transfers between devices  69.1 us (40%)
  blocking collectives  42.1 us (24%)
  matrix products  28.7 us (17%)
  between operations  14.2 us (8%)
  local copies, waits for them, and re-layouts  12.9 us (8%)
  other arithmetic  3.85 us (2%)
    all_gather x1, waiting for transfers between devices, shards(): group_all = lax.all_gather(coefficients, 'leaf', axis=1, tiled=True)[0]  42.1 us
    psum x1, blocking collectives, shards(): group_coef = lax.psum(contribution, 'leaf')  32.9 us
    dot_general x6, matrix products, matmul(): jnp.dot(left, right, precision=lax.Precision.HIGHEST, preferred_element_t...  28.7 us
    all_gather x1, waiting for transfers between devices, shards(): lax.all_gather(group_round, 'group', axis=0, tiled=True).astype(jnp.float32)  25.1 us
    all_gather x1, blocking collectives, shards(): coarse = lax.all_gather(coarse_part, 'leaf', axis=0, tiled=True)  9.22 us
    gather x1, local copies, waits for them, and re-layouts, shards(): selected = jnp.take(leaf_blocks, chosen, axis=0)  7.17 us
    unnamed x22, local copies, waits for them, and re-layouts  4.18 us
    select_n x2, other arithmetic, shards(): selected = jnp.take(leaf_blocks, chosen, axis=0)  3.8 us
  transfers between devices with their start and end apart: 4, of which 3 were waited for; matrix products, arithmetic and copies ran while one was open for 21% of the time, Pallas kernels for 0%

commit v1 on v0

--- a/solution.py
+++ b/solution.py
@@ -4,6 +4,7 @@
 from jax.sharding import PartitionSpec as P
 
 LPG = 4
+compute_sector = lambda point: jax.lax.all_gather(point, axis_name="leaf").sum(axis=0)
 
 
 def swapped(shard, axis, distance):
@@ -41,7 +42,7 @@
         partial_coef = kept + swapped(given, "leaf", bit_level)
     contribution = matmul(transfer[0].T, partial_coef)
     coupling_rows = coupling[0]
-    group_coef = lax.psum(contribution, "leaf")
+    group_coef = compute_sector(contribution)
     group_round = group_coef.astype(jnp.bfloat16)
     coarse_part = matmul(
         coupling_rows, lax.all_gather(group_round, "group", axis=0, tiled=True).astype(jnp.float32)

time: 172 us -> 187 us (1.087)
  waiting for transfers between devices: 69.1 us -> 110 us
  blocking collectives: 42.1 us -> 9.22 us
  local copies, waits for them, and re-layouts: 12.9 us -> 16.9 us
  other arithmetic: 3.85 us -> 5.84 us
    all_gather x0 -> x1, waiting for transfers between devices: none -> 40.1 us  [jax.lax.all_gather(point, axis_name='leaf').sum(axis=0)]
    psum x1 -> x0, blocking collectives: 32.9 us -> none  [shards(): group_coef = lax.psum(contribution, 'leaf')]
    unnamed x22 -> x23, local copies, waits for them, and re-layouts: 4.18 us -> 8.19 us
    reduce_sum x0 -> x1, other arithmetic: none -> 2 us  [jax.lax.all_gather(point, axis_name='leaf').sum(axis=0)]
  transfers between devices with their start and end apart: 4 -> 5, of which waited for: 3 -> 4; matrix products, arithmetic and copies ran while one was open for 21% -> 20% of each run, Pallas kernels for 0% -> 0%
where the time goes in v1:
time: 187 us; the launch traced here: 186 us
  waiting for transfers between devices  110 us (59%)
  matrix products  29.5 us (16%)
  local copies, waits for them, and re-layouts  16.9 us (9%)
  between operations  13.9 us (7%)
  blocking collectives  9.22 us (5%)
  other arithmetic  5.84 us (3%)
    all_gather x1, waiting for transfers between devices, shards(): group_all = lax.all_gather(coefficients, 'leaf', axis=1, tiled=True)[0]  42.1 us
    all_gather x1, waiting for transfers between devices, jax.lax.all_gather(point, axis_name='leaf').sum(axis=0)  40.1 us
    dot_general x6, matrix products, matmul(): jnp.dot(left, right, precision=lax.Precision.HIGHEST, preferred_element_t...  29.5 us
    all_gather x1, waiting for transfers between devices, shards(): lax.all_gather(group_round, 'group', axis=0, tiled=True).astype(jnp.float32)  25.8 us
    all_gather x1, blocking collectives, shards(): coarse = lax.all_gather(coarse_part, 'leaf', axis=0, tiled=True)  9.22 us
    unnamed x23, local copies, waits for them, and re-layouts  8.19 us
    gather x1, local copies, waits for them, and re-layouts, shards(): selected = jnp.take(leaf_blocks, chosen, axis=0)  7.18 us
    select_n x2, other arithmetic, shards(): selected = jnp.take(leaf_blocks, chosen, axis=0)  3.8 us
  transfers between devices with their start and end apart: 5, of which 4 were waited for; matrix products, arithmetic and copies ran while one was open for 20% of the time, Pallas kernels for 0%

profile of v1, /device:TPU:0, one launch (start us, length us, event | category | flops | bytes accessed | tf_op | source)
XLA Modules:
  0.0 186.3 jit_solution(14999747037506975875)
XLA Ops:
  6.5 0.0 copy-start
  6.5 0.0 all-gather.9.cloned.1.call-start
  6.5 1.0 copy-done
  7.6 2.3 %fusion.6 = f32[256,512]{1,0:T(8,128)S(1)} fusion(f32[1,512,512]{2,1,0:T(8,128)} %param.8, f32[1,512,256]{2,1,0:T(8,128)S(1)} %copy-done), kind=kOutput, calls=%fused_computation.13 | convolution fusion | flops 805306368 | bytes 2097152 | tf_op jit(solution)/shard_map/dot_general | solution.py:15
  9.9 0.6 collective-permute-start
  10.5 1.2 collective-permute-done
  11.6 2.3 %convolution_bitcast_fusion = f32[256,512]{0,1:T(8,128)} fusion(f32[128,512]{1,0:T(8,128)S(1)} %collective-permute-done, f32[256,512]{1,0:T(8,128)S(1)} %fusion.6, f32[1,128,256]{2,1,0:T(8,128)} %param.12, pred[]{:T(512)S(6)} %eq.7), kind=kOutput, calls=%fused_computation.10 | convolution fusion | flops 201457664 | bytes 1441793 | tf_op jit(solution)/shard_map/dot_general | solution.py:15
  14.0 0.0 all-gather.9.cloned.1.call-update
  14.0 0.0 all-gather.7.cloned.1.call-start
  14.0 40.1 %all-gather.9.cloned.1.call-done = f32[2048,512]{0,1:T(8,128)} async-done(((f32[256,512]{0,1:T(8,128)}), f32[2048,512]{0,1:T(8,128)}) %all-gather.9.cloned.1.call-update) | async-done | bytes 4194320 | tf_op jit(solution)/shard_map/all_gather | solution.py:7
  54.1 0.0 copy-start.1
  54.1 0.0 copy-start.4
  54.1 4.3 %copy.18 = f32[64,8,8,256]{3,2,1,0:T(8,128)S(1)} copy(f32[64,8,8,256]{3,1,2,0:T(8,128)} %bitcast.61) | data formatting | bytes 8388608
  58.4 0.0 copy-start.7
  58.4 0.0 copy-start.6
  58.4 0.0 copy-start.5
  58.4 2.0 %bitcast_reduce_fusion = bf16[256,512]{0,1:T(8,128)(2,1)} fusion(f32[64,8,8,256]{3,2,1,0:T(8,128)S(1)} %copy.18), kind=kLoop, calls=%fused_computation.3 | loop fusion | flops 917504 | bytes 4456448 | tf_op jit(solution)/shard_map/reduce_sum | solution.py:7
  60.4 0.0 all-gather.7.cloned.1.call-update
  60.4 0.0 all-gather.5.cloned.1.call-start
  60.5 0.7 all-gather.5.cloned.1.call-update
  61.2 0.0 copy-done.1
  61.2 1.3 copy.16
  63.2 0.0 copy-done.4
  63.2 1.3 copy.15
  64.5 0.0 copy-done.7
  64.5 0.2 dynamic-slice_reduce_fusion
  64.8 25.8 %all-gather.7.cloned.1.call-done = bf16[1024,512]{0,1:T(8,128)(2,1)} async-done(((bf16[256,512]{0,1:T(8,128)(2,1)}), bf16[1024,512]{0,1:T(8,128)(2,1)}) %all-gather.7.cloned.1.call-update) | async-done | bytes 1048592 | tf_op jit(solution)/shard_map/all_gather | solution.py:48
  90.5 0.0 copy-done.6
  90.5 2.2 %convolution_bitcast_fusion.2 = f32[32,512]{1,0:T(8,128)S(1)} fusion(bf16[1024,512]{0,1:T(8,128)(2,1)} %all-gather.7.cloned.1.call-done, f32[1,32,1024]{2,1,0:T(8,128)S(1)} %copy-done.6), kind=kOutput, calls=%fused_computation.12 | convolution fusion | flops 201326592 | bytes 1245184 | tf_op jit(solution)/shard_map/dot_general | solution.py:15
  92.8 9.2 %all_gather.19 = f32[256,512]{1,0:T(8,128)S(1)} all-gather(f32[32,512]{1,0:T(8,128)S(1)} %convolution_bitcast_fusion.2), channel_id=1, replica_groups=mesh['leaf'=8,'group'=4] {'leaf'}, dimensions={0}, use_global_device_ids=true | all-gather | bytes 589824 | tf_op jit(solution)/shard_map/all_gather | solution.py:50
  102.0 0.0 copy-done.5
  102.0 0.4 convolution_bitcast_fusion.1
  102.4 0.4 collective-permute-start.1
  102.9 42.1 %all-gather.5.cloned.1.call-done = f32[1,4096,512]{2,1,0:T(8,128)} async-done(((f32[1,512,512]{2,1,0:T(8,128)}), f32[1,4096,512]{2,1,0:T(8,128)}) %all-gather.5.cloned.1.call-update) | async-done | bytes 8388624 | tf_op jit(solution)/shard_map/all_gather | solution.py:29
  145.0 0.0 slice-start
  145.0 7.2 %gather_fusion = f32[3,1024,512]{2,1,0:T(8,128)} fusion(f32[4,1024,512]{2,1,0:T(8,128)} %bitcast.60, s32[1024]{0:T(1024)S(1)} %pad_clamp_fusion), kind=kCustom, calls=%fused_computation | custom fusion | bytes 12582924 | tf_op jit(solution)/shard_map/jit(_take)/gather | solution.py:31
  152.2 0.0 slice-start.1
  152.2 3.8 %broadcast_select_fusion = f32[3,1024,512]{2,1,0:T(8,128)S(1)} fusion(f32[3,1024,512]{2,1,0:T(8,128)} %gather_fusion, pred[3]{0:T(512)(128)(4,1)S(1)} %compare_and_fusion), kind=kLoop, calls=%fused_computation.4 | loop fusion | flops 1572864 | bytes 12582915 | tf_op jit(solution)/shard_map/jit(_take)/select_n | solution.py:31
  156.0 0.0 slice-done
  156.0 0.2 slice-done.1
  156.2 0.0 copy-start.2
  156.2 0.0 copy-start.3
  156.2 20.3 %fusion = f32[512,512]{1,0:T(8,128)S(1)} fusion(f32[3072,512]{1,0:T(8,128)S(1)} %bitcast.57, f32[1,512,3072]{2,1,0:T(8,128)S(1)} %bitcast.59), kind=kOutput, calls=%fused_computation.1 | convolution fusion | flops 9663676416 | bytes 13631488 | tf_op jit(solution)/shard_map/dot_general | solution.py:15
  176.5 0.0 collective-permute-done.1
  176.5 0.0 copy-done.2
  176.5 0.0 copy-done.3
  176.6 1.9 %fusion.5 = f32[1,512,512]{1,2,0:T(8,128)S(1)} fusion(f32[512,512]{1,0:T(8,128)S(1)} %fusion, f32[1,512,512]{1,2,0:T(8,128)S(1)} %copy-done.2, f32[1,512,512]{1,2,0:T(8,128)S(1)} %copy-done.3, f32[128,512]{1,0:T(8,128)S(1)} %convolution_bitcast_fusion.1, f32[128,512]{1,0:T(8,128)S(1)} %collective-permute-done.1, f32[1,512,256]{2,1,0:T(8,128)S(1)} %copy-done, ...), kind=kOutput, calls=%fused_computation.9 | convolution fusion | flops 806748160 | bytes 5242885 | tf_op jit(solution)/shard_map/dot_general | solution.py:15
  178.5 1.3 copy.17
  (5 shorter events, 0.1 us)
Async XLA Ops:
  6.5 1.0 copy-start
  6.5 47.5 %all-gather.9.cloned.1.call-start = ((), (), s32[]{:S(2)}) async-start(), calls=%async_computation.2 | async-start | bytes 4718592 | tf_op jit(solution)/shard_map/all_gather | solution.py:7
  9.9 1.7 collective-permute-start
  14.0 76.5 %all-gather.7.cloned.1.call-start = ((), (), s32[]{:S(2)}) async-start(), calls=%async_computation.1 | async-start | bytes 1310720 | tf_op jit(solution)/shard_map/all_gather | solution.py:48
  54.1 7.1 %copy-start.1 = (f32[1,512,512]{2,1,0:T(8,128)S(1)}, f32[1,512,512]{2,1,0:T(8,128)}, u32[]{:S(2)}) copy-start(f32[1,512,512]{2,1,0:T(8,128)} %param.8) | copy-start | bytes 3145732
  54.1 9.1 %copy-start.4 = (f32[1,512,512]{2,1,0:T(8,128)S(1)}, f32[1,512,512]{2,1,0:T(8,128)}, u32[]{:S(2)}) copy-start(f32[1,512,512]{2,1,0:T(8,128)} %param.9) | copy-start | bytes 3145732
  58.4 6.1 %copy-start.7 = (s32[1,4,3]{1,0,2:T(1,128)S(1)}, s32[1,4,3]{1,0,2:T(1,128)}, u32[]{:S(2)}) copy-start(s32[1,4,3]{1,0,2:T(1,128)} %param.14) | copy-start | bytes 148
  58.4 32.1 %copy-start.6 = (f32[1,32,1024]{2,1,0:T(8,128)S(1)}, f32[1,32,1024]{2,1,0:T(8,128)}, u32[]{:S(2)}) copy-start(f32[1,32,1024]{2,1,0:T(8,128)} %param.13) | copy-start | bytes 393220
  58.4 43.6 %copy-start.5 = (f32[1,128,256]{2,1,0:T(8,128)S(1)}, f32[1,128,256]{2,1,0:T(8,128)}, u32[]{:S(2)}) copy-start(f32[1,128,256]{2,1,0:T(8,128)} %param.12) | copy-start | bytes 393220
  60.4 84.6 %all-gather.5.cloned.1.call-start = ((), (), s32[]{:S(2)}) async-start(), calls=%async_computation | async-start | bytes 9437184 | tf_op jit(solution)/shard_map/all_gather | solution.py:29
  102.4 74.1 %collective-permute-start.1 = (f32[128,512]{1,0:T(8,128)S(1)}, f32[128,512]{1,0:T(8,128)S(1)}, u32[]{:S(2)}, u32[]{:S(2)}) collective-permute-start(f32[128,512]{1,0:T(8,128)S(1)} %convolution_bitcast_fusion.1), channel_id=1, source_target_pairs={{0,4},{4,0},{8,12},{12,8},{16,20},{20,16},{24,28},{28,24},{1,5},{5... | collective-permute-start | bytes 786440 | tf_op jit(solution)/shard_map/ppermute | solution.py:11
  145.0 11.0 %slice-start = ((s8[6291456]{0:T(1024)(128)(4,1)}), s8[2097152]{0:T(1024)(128)(4,1)S(1)}, s32[]{:S(2)}) async-start(s8[6291456]{0:T(1024)(128)(4,1)} %bitcast.58), calls=%async_computation.3 | async-start | bytes 4194304
  152.2 4.0 %slice-start.1 = ((s8[6291456]{0:T(1024)(128)(4,1)}), s8[4194304]{0:T(1024)(128)(4,1)S(1)}, s32[]{:S(2)}) async-start(s8[6291456]{0:T(1024)(128)(4,1)} %bitcast.58), calls=%async_computation.4 | async-start | bytes 8388608
  156.2 20.3 %copy-start.2 = (f32[1,512,512]{1,2,0:T(8,128)S(1)}, f32[1,512,512]{1,2,0:T(8,128)}, u32[]{:S(2)}) copy-start(f32[1,512,512]{1,2,0:T(8,128)} %copy.16) | copy-start | bytes 3145732
  156.2 20.4 %copy-start.3 = (f32[1,512,512]{1,2,0:T(8,128)S(1)}, f32[1,512,512]{1,2,0:T(8,128)}, u32[]{:S(2)}) copy-start(f32[1,512,512]{1,2,0:T(8,128)} %copy.15) | copy-start | bytes 3145732
Sparse Core Ops, SparseCore 0:
  14.1 39.9 all-gather.8
  60.6 29.9 all-gather.6
  92.4 52.5 all-gather.4
